TPU v7x, 32 devices: a whole 2x2x4 slice. The times are simulated.
32 devices in a mesh: dp: 2 (over y), seq: 16 (over z, x, core).
Axes of the slice: x: 2, y: 2, z: 4, core: 2. Of those that a mesh axis runs over, the one named last changes fastest.
Arguments:
- features: bfloat16 [4096, 320], P(('dp', 'seq')), parts along dimension 0, may hold values from -40 to 40
- hint: bfloat16 [4096, 320], P(('dp', 'seq')), parts along dimension 0, may hold values from -6 to 6
- conv_weight: bfloat16 [3, 3, 320, 320], replicated, may hold values from -0.109375 to 0.109375
- conv_bias: float32 [320], replicated, may hold values from -3 to 3
- zero_weight: bfloat16 [320, 320], replicated, may hold values from -0.3125 to 0.3125
- zero_bias: float32 [320], replicated, may hold values from -2 to 2
- group_gain: float32 [320], replicated, may hold values from 0.5 to 1.5
- proj_in: bfloat16 [320, 320], replicated, may hold values from -0.3125 to 0.3125
- norm_gain: float32 [320], replicated, may hold values from 0.5 to 1.5
- query_weight: bfloat16 [320, 320], replicated, may hold values from -2 to 2
- key_weight: bfloat16 [320, 320], replicated, may hold values from -2 to 2
- value_weight: bfloat16 [320, 320], replicated, may hold values from -0.3125 to 0.3125
- attn_out: bfloat16 [320, 320], replicated, may hold values from -0.3125 to 0.3125
- proj_out: bfloat16 [320, 320], replicated, may hold values from -0.3125 to 0.3125
Outputs:
- block_out: bfloat16 [4096, 320], P(('dp', 'seq')), parts along dimension 0
There are 2 independent parts, one for each index of `dp`. A program takes and returns all parts, laid end to end along the dimension named above; an argument that names none is the same for every part. Nothing has to cross between parts.
All inputs are finite; a program needn't handle non-finite values.
Results may differ from a plain program's by a relative error of at most 0.023.
Values may be sent and summed in bfloat16 or wider, within the bound.
A program may use at most 64 MiB of HBM per device.

v0:
```python
import math
import jax
import jax.numpy as jnp
from jax import lax
from jax.sharding import PartitionSpec as P

HEADS = 8
GROUPS = 32
WIDTH = 128
norm_eps = 1e-06
layer_eps = 1e-05


def with_halo(block, sides, width):
    for axis, dim in sides:
        count = lax.axis_size(axis)
        forward = [(i, i + 1) for i in range(count - 1)]
        backward = [(target, source) for source, target in forward]
        low = lax.ppermute(
            lax.slice_in_dim(block, block.shape[dim] - width, None, axis=dim), axis, forward
        )
        high = lax.ppermute(lax.slice_in_dim(block, 0, width, axis=dim), axis, backward)
        block = jnp.concatenate([low, block, high], axis=dim)
    return block


def conv_extended(extended, conv_weight, conv_bias, width):
    line_count = extended.shape[0] // width - 2
    channels = extended.shape[1]
    lattice = extended.reshape(line_count + 2, width, channels)
    padded = jnp.pad(lattice, ((0, 0), (1, 1), (0, 0)))
    summed = jnp.zeros((line_count * width, conv_weight.shape[3]), jnp.float32)
    for row_shift in range(3):
        for col_shift in range(3):
            window = padded[row_shift : row_shift + line_count, col_shift : col_shift + width]
            window = window.reshape(line_count * width, channels)
            summed = summed + jnp.dot(
                window, conv_weight[row_shift, col_shift], preferred_element_type=jnp.float32
            )
    return summed + conv_bias


def fold_blocks(carry_in, queries, pieces, make_pairs):
    row_total = pieces[0].shape[0]
    block_len = math.gcd(row_total, 1024)
    stacked = tuple(
        (member.reshape(row_total // block_len, block_len, member.shape[1]) for member in pieces)
    )
    score_scale = 1.0 / math.sqrt(queries.shape[2])

    def advance(carry_now, slab_rows):
        running_max, running_sum, weighted = carry_now
        keys_block, values_block = make_pairs(slab_rows)
        scores = (
            jnp.einsum("qhd,khd->hqk", queries, keys_block, preferred_element_type=jnp.float32)
            * score_scale
        )
        new_max = jnp.maximum(running_max, jnp.max(scores, axis=2))
        decay_by = jnp.exp(running_max - new_max)
        weights = jnp.exp(scores - new_max[:, :, None])
        running_sum = running_sum * decay_by + jnp.sum(weights, axis=2)
        weighted = weighted * jnp.transpose(decay_by)[:, :, None] + jnp.einsum(
            "hqk,khd->qhd",
            weights.astype(jnp.bfloat16),
            values_block,
            preferred_element_type=jnp.float32,
        )
        return ((new_max, running_sum, weighted), None)

    carry_out, unused = lax.scan(advance, carry_in, stacked)
    return carry_out


def local(
    features,
    hint,
    conv_weight,
    conv_bias,
    zero_weight,
    zero_bias,
    group_gain,
    proj_in,
    norm_gain,
    query_weight,
    key_weight,
    value_weight,
    attn_out,
    proj_out,
):
    tok_count, channels = features.shape
    head_dim = channels // HEADS
    extended = with_halo(hint, (("seq", 0),), WIDTH)
    control = jax.nn.silu(conv_extended(extended, conv_weight, conv_bias, WIDTH)).astype(
        jnp.bfloat16
    )
    branch = jnp.dot(control, zero_weight, preferred_element_type=jnp.float32) + zero_bias
    merged = (features.astype(jnp.float32) + branch).astype(jnp.bfloat16)
    widened = merged.astype(jnp.float32)
    per_group = channels // GROUPS
    entry_count = tok_count * lax.axis_size("seq") * per_group
    local_sum = jnp.sum(widened.reshape(tok_count, GROUPS, per_group), axis=(0, 2))
    mean_group = lax.psum(local_sum, "seq") / entry_count
    centred = widened - jnp.repeat(mean_group, per_group)
    local_spread = jnp.sum(jnp.square(centred).reshape(tok_count, GROUPS, per_group), axis=(0, 2))
    var_group = lax.psum(local_spread, "seq") / entry_count
    mean_chan = jnp.repeat(mean_group, per_group)
    inv_chan = jnp.repeat(lax.rsqrt(var_group + norm_eps), per_group)
    grouped = ((widened - mean_chan) * inv_chan * group_gain).astype(jnp.bfloat16)
    inner_rows = jnp.dot(grouped, proj_in, preferred_element_type=jnp.float32).astype(jnp.bfloat16)
    inner_wide = inner_rows.astype(jnp.float32)
    centre = jnp.mean(inner_wide, axis=1, keepdims=True)
    spread = jnp.mean(jnp.square(inner_wide - centre), axis=1, keepdims=True)
    normed = ((inner_wide - centre) * lax.rsqrt(spread + layer_eps) * norm_gain).astype(
        jnp.bfloat16
    )
    queries = jnp.dot(normed, query_weight, preferred_element_type=jnp.float32).astype(jnp.bfloat16)
    queries = queries.reshape(tok_count, HEADS, head_dim)
    group_span = lax.axis_size("seq") // HEADS
    sub_rows = tok_count // group_span
    local_keys = jnp.dot(normed, key_weight, preferred_element_type=jnp.float32).astype(
        jnp.bfloat16
    )
    local_values = jnp.dot(normed, value_weight, preferred_element_type=jnp.float32).astype(
        jnp.bfloat16
    )
    query_send = (
        queries.reshape(group_span, sub_rows, HEADS, head_dim)
        .transpose(2, 0, 1, 3)
        .reshape(HEADS * group_span, sub_rows, head_dim)
    )

    def copies_for(matrix):
        by_head = matrix.reshape(tok_count, HEADS, head_dim).transpose(1, 0, 2)
        return jnp.broadcast_to(by_head[:, None], (HEADS, group_span, tok_count, head_dim)).reshape(
            HEADS * group_span, tok_count, head_dim
        )

    own_queries = lax.all_to_all(query_send, "seq", split_axis=0, concat_axis=0, tiled=True)
    head_keys, head_values = (
        lax.all_to_all(copies_for(local_keys), "seq", split_axis=0, concat_axis=0, tiled=True),
        lax.all_to_all(copies_for(local_values), "seq", split_axis=0, concat_axis=0, tiled=True),
    )
    query_rows = own_queries.shape[0] * sub_rows
    own_queries = own_queries.reshape(query_rows, 1, head_dim)
    key_rows = head_keys.reshape(-1, head_dim)
    value_rows = head_values.reshape(-1, head_dim)

    def single_pairs(slab_rows):
        return (slab_rows[0].reshape(-1, 1, head_dim), slab_rows[1].reshape(-1, 1, head_dim))

    head_carry = (
        jnp.full((1, query_rows), -1e30, jnp.float32),
        jnp.zeros((1, query_rows), jnp.float32),
        jnp.zeros((query_rows, 1, head_dim), jnp.float32),
    )
    running_max, running_sum, weighted = fold_blocks(
        head_carry, own_queries, (key_rows, value_rows), single_pairs
    )
    head_result = (weighted / jnp.transpose(running_sum)[:, :, None]).astype(jnp.bfloat16)
    head_result = head_result.reshape(lax.axis_size("seq"), sub_rows, head_dim)
    returned = lax.all_to_all(head_result, "seq", split_axis=0, concat_axis=0, tiled=True)
    attended = (
        returned.reshape(HEADS, group_span, sub_rows, head_dim)
        .transpose(1, 2, 0, 3)
        .reshape(tok_count, channels)
    )
    after_attn = (
        inner_wide + jnp.dot(attended, attn_out, preferred_element_type=jnp.float32)
    ).astype(jnp.bfloat16)
    return (widened + jnp.dot(after_attn, proj_out, preferred_element_type=jnp.float32)).astype(
        jnp.bfloat16
    )


def solution(mesh):
    placed = (
        P(("dp", "seq"), None),
        P(("dp", "seq"), None),
        P(),
        P(),
        P(),
        P(),
        P(),
        P(),
        P(),
        P(),
        P(),
        P(),
        P(),
        P(),
    )
    return jax.shard_map(
        local, mesh=mesh, in_specs=placed, out_specs=P(("dp", "seq"), None), check_vma=False
    )
```

profile of v0, /device:TPU:0, one launch (start us, length us, event | category | flops | bytes accessed | tf_op | source)
XLA Modules:
  0.0 143.6 jit_solution(5059006337217862261)
XLA Ops:
  0.0 2.7 %collective-permute-start = (bf16[128,320]{0,1:T(8,128)(2,1)}, bf16[128,320]{0,1:T(8,128)(2,1)S(1)}, u32[]{:S(2)}, u32[]{:S(2)}) collective-permute-start(bf16[128,320]{0,1:T(8,128)(2,1)} %param.17), channel_id=1, source_target_pairs={{0,1},{1,2},{2,3},{3,4},{4,5},{5,6},{6,7},{7,8},{8,9},{9,10},{10,1... | collective-permute-start | bytes 245768 | tf_op jit(solution)/shard_map/ppermute | solution.py:19
  2.7 1.3 collective-permute-start.1
  4.0 4.2 %collective-permute-done.1 = bf16[128,320]{0,1:T(8,128)(2,1)S(1)} collective-permute-done((bf16[128,320]{0,1:T(8,128)(2,1)}, bf16[128,320]{0,1:T(8,128)(2,1)S(1)}, u32[]{:S(2)}, u32[]{:S(2)}) %collective-permute-start.1) | collective-permute-done | bytes 81952 | tf_op jit(solution)/shard_map/ppermute | solution.py:22
  8.1 1.0 pad_maximum_fusion
  9.1 0.2 copy.64
  9.3 1.2 fusion.39
  10.6 1.9 %fusion.30 = f32[128,320]{0,1:T(8,128)} fusion(bf16[3,3,320,320]{3,2,1,0:T(8,128)(2,1)} %param.18, bf16[3,128,320]{2,1,0:T(8,128)(2,1)S(1)} %bitcast.143), kind=kOutput, calls=%fused_computation.46 | convolution fusion | flops 26214400 | bytes 655360 | tf_op jit(solution)/shard_map/dot_general | solution.py:37
  12.5 0.3 convolution_add_fusion.9
  12.8 0.3 convolution_add_fusion.8
  13.1 0.3 convolution_add_fusion.7
  13.4 0.3 convolution_add_fusion.6
  13.7 0.3 convolution_add_fusion.5
  14.0 0.9 convolution_add_fusion.4
  15.0 1.7 %fusion.78 = (f32[320]{0:T(512)S(1)}, f32[128,320]{0,1:T(8,128)S(1)}) fusion(f32[320]{0:T(512)S(1)} %copy-done.13, bf16[320,320]{1,0:T(8,128)(2,1)S(1)} %copy-done, f32[128,320]{0,1:T(8,128)} %fusion.30, f32[128,320]{0,1:T(8,128)} %convolution_add_fusion.4, bf16[128,320]{0,1:T(8,128)(2,1)} %copy-done.10, bf16[3,3,320,320]{3,2,1,0:T(8,128)(2,1)S(1)} %copy-done.2, ...), kind=kOutput, calls=%fused_computation.100 | convolution fusion | flops 53001920 | bytes 1152256 | tf_op jit(solution)/shard_map/dot_general | solution.py:96
  16.9 32.7 %psum.14 = f32[32]{0:T(128)S(1)} all-reduce(f32[32]{0:T(128)S(1)} %reduce_sum.63), channel_id=1, replica_groups=mesh['dp'=2,'seq'=16] {'seq'}, use_global_device_ids=true, to_apply=%region_2.3 | all-reduce | flops 32 | bytes 256 | tf_op jit(solution)/shard_map/psum | solution.py:102
  49.8 0.2 multiply_reduce_fusion.2
  50.2 29.5 %psum.15 = f32[32]{0:T(128)S(1)} all-reduce(f32[32]{0:T(128)S(1)} %reduce_sum.66), channel_id=1, replica_groups=mesh['dp'=2,'seq'=16] {'seq'}, use_global_device_ids=true, to_apply=%region_5.6 | all-reduce | flops 32 | bytes 256 | tf_op jit(solution)/shard_map/psum | solution.py:105
  80.0 0.5 fusion.81
  80.7 0.3 convolution_convert_fusion.1
  81.1 0.8 reshape.134
  81.9 3.5 %all-to-all-start.1 = ((bf16[16,2,1280]{2,1,0:T(2,128)(2,1)}), bf16[16,2,1280]{2,1,0:T(2,128)(2,1)S(1)}, u32[]{:S(2)}, u32[]{:S(2)}) async-start(bf16[16,2,1280]{2,1,0:T(2,128)(2,1)} %reshape.134), calls=%async_computation.1 | async-start | bytes 163840 | tf_op jit(solution)/shard_map/all_to_all | solution.py:138
  85.4 0.3 convolution_convert_fusion.2
  85.7 6.8 %all-to-all-done.1 = bf16[16,2,1280]{2,1,0:T(2,128)(2,1)S(1)} async-done(((bf16[16,2,1280]{2,1,0:T(2,128)(2,1)}), bf16[16,2,1280]{2,1,0:T(2,128)(2,1)S(1)}, u32[]{:S(2)}, u32[]{:S(2)}) %all-to-all-start.1) | async-done | bytes 81952 | tf_op jit(solution)/shard_map/all_to_all | solution.py:138
  92.5 0.7 broadcast_in_dim.19
  93.2 3.5 %all-to-all-start = ((bf16[16,128,40]{1,2,0:T(8,128)(2,1)}), bf16[16,128,40]{1,2,0:T(8,128)(2,1)S(1)}, u32[]{:S(2)}, u32[]{:S(2)}) async-start(bf16[16,128,40]{1,2,0:T(8,128)(2,1)} %bitcast.18), calls=%async_computation | async-start | bytes 327680 | tf_op jit(solution)/shard_map/all_to_all | solution.py:140
  96.7 0.3 convolution_convert_fusion
  97.0 8.1 %all-to-all-done = bf16[16,128,40]{1,2,0:T(8,128)(2,1)S(1)} async-done(((bf16[16,128,40]{1,2,0:T(8,128)(2,1)}), bf16[16,128,40]{1,2,0:T(8,128)(2,1)S(1)}, u32[]{:S(2)}, u32[]{:S(2)}) %all-to-all-start) | async-done | bytes 163872 | tf_op jit(solution)/shard_map/all_to_all | solution.py:140
  105.1 0.7 broadcast_in_dim.20
  105.8 3.5 %all-to-all-start.2 = ((bf16[16,128,40]{1,2,0:T(8,128)(2,1)}), bf16[16,128,40]{1,2,0:T(8,128)(2,1)S(1)}, u32[]{:S(2)}, u32[]{:S(2)}) async-start(bf16[16,128,40]{1,2,0:T(8,128)(2,1)} %bitcast.24), calls=%async_computation.2 | async-start | bytes 327680 | tf_op jit(solution)/shard_map/all_to_all | solution.py:141
  109.3 0.2 reshape.135
  109.5 0.2 reshape.125
  109.7 0.3 copy.79
  110.0 7.7 %all-to-all-done.2 = bf16[16,128,40]{1,2,0:T(8,128)(2,1)S(1)} async-done(((bf16[16,128,40]{1,2,0:T(8,128)(2,1)}), bf16[16,128,40]{1,2,0:T(8,128)(2,1)S(1)}, u32[]{:S(2)}, u32[]{:S(2)}) %all-to-all-start.2) | async-done | bytes 163872 | tf_op jit(solution)/shard_map/all_to_all | solution.py:141
  117.7 0.3 copy.80
  118.0 13.9 %while.15 = (s32[]{:T(128)}, f32[1,1024]{1,0:T(1,128)S(1)}, f32[1,1024]{1,0:T(1,128)S(1)}, f32[1024,1,40]{0,2,1:T(8,128)S(1)}, bf16[2,1024,40]{2,1,0:T(8,128)(2,...) while((s32[]{:T(128)}, f32[1,1024]{1,0:T(1,128)S(1)}, ...), condition=%wide.region_11.12_spmd.clone, body=%wide.region_8.0_spmd.clone.sunk | while | flops 176288768 | bytes 30359692 | solution.py:70
  118.0 2.6 %multiply_reduce_fusion.4 = (f32[1024]{0:T(1024)S(1)}, f32[1024,1024]{1,0:T(8,128)}) fusion(bf16[1024,1,40]{0,2,1:T(8,128)(2,1)S(1)} %get-tuple-element.172, bf16[2,1024,40]{2,1,0:T(8,128)(2,1)S(1)} %get-tuple-element.171, s32[]{:T(128)} %get-tuple-element.158), kind=kOutput, calls=%fused_computation.1.clone.1 | convolution fusion | flops 85982208 | bytes 4542468 | tf_op jit(solution)/shard_map/while/body/eval_jaxpr/qhd,khd->hqk/dot_general | solution.py:55
  120.7 3.1 %fusion.105 = f32[1024]{0:T(1024)S(1)} fusion(f32[1024,1024]{1,0:T(8,128)} %get-tuple-element.146, f32[1024]{0:T(1024)S(1)} %bitcast.150), kind=kLoop, calls=%fused_computation.3.clone.1 | loop fusion | flops 3144704 | bytes 4202496 | tf_op jit(solution)/shard_map/while/body/eval_jaxpr/reduce_sum | solution.py:61
  123.8 0.3 copy-done.1
  124.1 0.8 fusion.107
  125.0 2.6 %multiply_reduce_fusion.4 = (f32[1024]{0:T(1024)S(1)}, f32[1024,1024]{1,0:T(8,128)}) fusion(bf16[1024,1,40]{0,2,1:T(8,128)(2,1)S(1)} %get-tuple-element.172, bf16[2,1024,40]{2,1,0:T(8,128)(2,1)S(1)} %get-tuple-element.171, s32[]{:T(128)} %get-tuple-element.158), kind=kOutput, calls=%fused_computation.1.clone.1 | convolution fusion | flops 85982208 | bytes 4542468 | tf_op jit(solution)/shard_map/while/body/eval_jaxpr/qhd,khd->hqk/dot_general | solution.py:55
  127.6 3.1 %fusion.105 = f32[1024]{0:T(1024)S(1)} fusion(f32[1024,1024]{1,0:T(8,128)} %get-tuple-element.146, f32[1024]{0:T(1024)S(1)} %bitcast.150), kind=kLoop, calls=%fused_computation.3.clone.1 | loop fusion | flops 3144704 | bytes 4202496 | tf_op jit(solution)/shard_map/while/body/eval_jaxpr/reduce_sum | solution.py:61
  130.7 0.3 copy-done.1
  131.0 0.8 fusion.107
  132.0 0.2 reshape.128
  132.2 0.2 reshape.136
  132.3 9.7 %all_to_all.20 = bf16[16,2,1280]{2,1,0:T(2,128)(2,1)S(1)} all-to-all(bf16[16,2,1280]{2,1,0:T(2,128)(2,1)S(1)} %reshape.136), channel_id=1, replica_groups=mesh['dp'=2,'seq'=16] {'seq'}, dimensions={0} | all-to-all | bytes 163840 | tf_op jit(solution)/shard_map/all_to_all | solution.py:161
  142.0 0.2 reshape.137
  142.5 1.1 fusion.28
  (61 shorter events, 1.6 us)
Async XLA Ops:
  0.0 15.0 %copy-start = (bf16[320,320]{1,0:T(8,128)(2,1)S(1)}, bf16[320,320]{1,0:T(8,128)(2,1)}, u32[]{:S(2)}) copy-start(bf16[320,320]{1,0:T(8,128)(2,1)} %param.20) | copy-start | bytes 614404
  0.0 12.5 %copy-start.2 = (bf16[3,3,320,320]{3,2,1,0:T(8,128)(2,1)S(1)}, bf16[3,3,320,320]{3,2,1,0:T(8,128)(2,1)}, u32[]{:S(2)}) copy-start(bf16[3,3,320,320]{3,2,1,0:T(8,128)(2,1)} %param.18) | copy-start | bytes 5529604
  0.0 4.0 %collective-permute-start = (bf16[128,320]{0,1:T(8,128)(2,1)}, bf16[128,320]{0,1:T(8,128)(2,1)S(1)}, u32[]{:S(2)}, u32[]{:S(2)}) collective-permute-start(bf16[128,320]{0,1:T(8,128)(2,1)} %param.17), channel_id=1, source_target_pairs={{0,1},{1,2},{2,3},{3,4},{4,5},{5,6},{6,7},{7,8},{8,9},{9,10},{10,1... | collective-permute-start | bytes 245768 | tf_op jit(solution)/shard_map/ppermute | solution.py:19
  2.7 5.5 %collective-permute-start.1 = (bf16[128,320]{0,1:T(8,128)(2,1)}, bf16[128,320]{0,1:T(8,128)(2,1)S(1)}, u32[]{:S(2)}, u32[]{:S(2)}) collective-permute-start(bf16[128,320]{0,1:T(8,128)(2,1)} %param.17), channel_id=1, source_target_pairs={{1,0},{2,1},{3,2},{4,3},{5,4},{6,5},{7,6},{8,7},{9,8},{10,9},{11,1... | collective-permute-start | bytes 245768 | tf_op jit(solution)/shard_map/ppermute | solution.py:22
  8.1 1.2 copy-start.10
  9.1 4.3 %copy-start.3 = (bf16[128,320]{0,1:T(8,128)(2,1)S(1)}, bf16[128,320]{0,1:T(8,128)(2,1)}, u32[]{:S(2)}) copy-start(bf16[128,320]{0,1:T(8,128)(2,1)} %param.17) | copy-start | bytes 245764
  12.8 2.2 %copy-start.13 = (f32[320]{0:T(512)S(1)}, f32[320]{0:T(512)}, u32[]{:S(2)}) copy-start(f32[320]{0:T(512)} %param.21) | copy-start | bytes 3844
  12.8 2.2 %copy-start.14 = (f32[320]{0:T(512)S(1)}, f32[320]{0:T(512)}, u32[]{:S(2)}) copy-start(f32[320]{0:T(512)} %param.19) | copy-start | bytes 3844
  13.4 66.6 %copy-start.4 = (bf16[320,320]{1,0:T(8,128)(2,1)S(1)}, bf16[320,320]{1,0:T(8,128)(2,1)}, u32[]{:S(2)}) copy-start(bf16[320,320]{1,0:T(8,128)(2,1)} %param.23) | copy-start | bytes 614404
  13.4 66.6 %copy-start.11 = (f32[320]{0:T(512)S(1)}, f32[320]{0:T(512)}, u32[]{:S(2)}) copy-start(f32[320]{0:T(512)} %param.22) | copy-start | bytes 3844
  13.7 66.8 %copy-start.12 = (f32[320]{0:T(512)S(1)}, f32[320]{0:T(512)}, u32[]{:S(2)}) copy-start(f32[320]{0:T(512)} %param.24) | copy-start | bytes 3844
  13.7 66.9 %copy-start.5 = (bf16[320,320]{1,0:T(8,128)(2,1)S(1)}, bf16[320,320]{1,0:T(8,128)(2,1)}, u32[]{:S(2)}) copy-start(bf16[320,320]{1,0:T(8,128)(2,1)} %param.25) | copy-start | bytes 614404
  15.0 70.5 %copy-start.6 = (bf16[320,320]{1,0:T(8,128)(2,1)S(1)}, bf16[320,320]{1,0:T(8,128)(2,1)}, u32[]{:S(2)}) copy-start(bf16[320,320]{1,0:T(8,128)(2,1)} %param.26) | copy-start | bytes 614404
  16.7 80.0 %copy-start.7 = (bf16[320,320]{1,0:T(8,128)(2,1)S(1)}, bf16[320,320]{1,0:T(8,128)(2,1)}, u32[]{:S(2)}) copy-start(bf16[320,320]{1,0:T(8,128)(2,1)} %param.27) | copy-start | bytes 614404
  81.9 10.6 %all-to-all-start.1 = ((bf16[16,2,1280]{2,1,0:T(2,128)(2,1)}), bf16[16,2,1280]{2,1,0:T(2,128)(2,1)S(1)}, u32[]{:S(2)}, u32[]{:S(2)}) async-start(bf16[16,2,1280]{2,1,0:T(2,128)(2,1)} %reshape.134), calls=%async_computation.1 | async-start | bytes 163840 | tf_op jit(solution)/shard_map/all_to_all | solution.py:138
  93.2 11.9 %all-to-all-start = ((bf16[16,128,40]{1,2,0:T(8,128)(2,1)}), bf16[16,128,40]{1,2,0:T(8,128)(2,1)S(1)}, u32[]{:S(2)}, u32[]{:S(2)}) async-start(bf16[16,128,40]{1,2,0:T(8,128)(2,1)} %bitcast.18), calls=%async_computation | async-start | bytes 327680 | tf_op jit(solution)/shard_map/all_to_all | solution.py:140
  105.8 11.9 %all-to-all-start.2 = ((bf16[16,128,40]{1,2,0:T(8,128)(2,1)}), bf16[16,128,40]{1,2,0:T(8,128)(2,1)S(1)}, u32[]{:S(2)}, u32[]{:S(2)}) async-start(bf16[16,128,40]{1,2,0:T(8,128)(2,1)} %bitcast.24), calls=%async_computation.2 | async-start | bytes 327680 | tf_op jit(solution)/shard_map/all_to_all | solution.py:141
  120.7 3.4 %copy-start.1 = (f32[1024,1024]{1,0:T(8,128)S(1)}, f32[1024,1024]{1,0:T(8,128)}, u32[]{:S(2)}) copy-start(f32[1024,1024]{1,0:T(8,128)} %get-tuple-element.146) | copy-start | bytes 12582916 | tf_op jit(solution)/shard_map/while
  127.6 3.4 %copy-start.1 = (f32[1024,1024]{1,0:T(8,128)S(1)}, f32[1024,1024]{1,0:T(8,128)}, u32[]{:S(2)}) copy-start(f32[1024,1024]{1,0:T(8,128)} %get-tuple-element.146) | copy-start | bytes 12582916 | tf_op jit(solution)/shard_map/while
  131.9 10.6 %copy-start.8 = (bf16[320,320]{1,0:T(8,128)(2,1)S(1)}, bf16[320,320]{1,0:T(8,128)(2,1)}, u32[]{:S(2)}) copy-start(bf16[320,320]{1,0:T(8,128)(2,1)} %param.29) | copy-start | bytes 614404
  131.9 10.6 %copy-start.9 = (bf16[320,320]{1,0:T(8,128)(2,1)S(1)}, bf16[320,320]{1,0:T(8,128)(2,1)}, u32[]{:S(2)}) copy-start(bf16[320,320]{1,0:T(8,128)(2,1)} %param.28) | copy-start | bytes 614404
where the time goes:
time: 144 us
  blocking collectives  71.9 us (50%)
  waiting for transfers between devices  26.7 us (19%)
  matrix products  16.6 us (12%)
  starting transfers between devices  14.5 us (10%)
  other arithmetic  7.84 us (5%)
  local copies, waits for them, and re-layouts  5.58 us (4%)
    psum x1, blocking collectives, local(): mean_group = lax.psum(local_sum, 'seq') / entry_count  32.7 us
    psum x1, blocking collectives, local(): var_group = lax.psum(local_spread, 'seq') / entry_count  29.5 us
    all_to_all x1, blocking collectives, local(): lax.all_to_all(head_result, 'seq', split_axis=0, concat_axis=0, tiled=True)  9.7 us
    all_to_all x1, waiting for transfers between devices, local(): lax.all_to_all(copies_for(local_keys), 'seq', split_axis=0, concat_axis=0...  8.08 us
    all_to_all x1, waiting for transfers between devices, local(): lax.all_to_all(copies_for(local_values), 'seq', split_axis=0, concat_axis...  7.68 us
    all_to_all x1, waiting for transfers between devices, local(): lax.all_to_all(query_send, 'seq', split_axis=0, concat_axis=0, tiled=True)  6.76 us
    reduce_sum x2, other arithmetic, advance(): running_sum = running_sum * decay_by + jnp.sum(weights, axis=2)  6.15 us
    dot_general x8, matrix products, conv_extended(): jnp.dot(window, conv_weight[row_shift, col_shift], preferred_element_type...  5.47 us
  transfers between devices with their start and end apart: 5, of which 4 were waited for; matrix products, arithmetic and copies ran while one was open for 1% of the time, Pallas kernels for 0%

commit v1 on v0

--- a/solution.py
+++ b/solution.py
@@ -9,6 +9,28 @@
 WIDTH = 128
 norm_eps = 1e-06
 layer_eps = 1e-05
+
+
+def in_blocks(x, dim, peers):
+    before, after = (x.shape[:dim], x.shape[dim + 1 :])
+    return jnp.moveaxis(x.reshape(*before, peers, -1, *after), dim, 0)
+
+
+def laid_out(blocks, dim):
+    lengths = list(blocks.shape[1:])
+    lengths[dim] *= blocks.shape[0]
+    return jnp.moveaxis(blocks, 0, dim).reshape(lengths)
+
+
+def swapped_with_each(array, axis, split_dim, concat_dim):
+    size, mine = (lax.axis_size(axis), lax.axis_index(axis))
+    tiles = in_blocks(array, split_dim, size)
+    outs = [tiles[mine]]
+    for step in range(1, size):
+        sent = tiles[mine ^ step]
+        outs.append(lax.ppermute(sent, axis, [(i, i ^ step) for i in range(size)]))
+    tiles = jnp.stack(outs)[mine ^ jnp.arange(size)]
+    return laid_out(tiles, concat_dim)
 
 
 def with_halo(block, sides, width):
@@ -138,7 +160,7 @@
     own_queries = lax.all_to_all(query_send, "seq", split_axis=0, concat_axis=0, tiled=True)
     head_keys, head_values = (
         lax.all_to_all(copies_for(local_keys), "seq", split_axis=0, concat_axis=0, tiled=True),
-        lax.all_to_all(copies_for(local_values), "seq", split_axis=0, concat_axis=0, tiled=True),
+        swapped_with_each(copies_for(local_values), "seq", 0, 0),
     )
     query_rows = own_queries.shape[0] * sub_rows
     own_queries = own_queries.reshape(query_rows, 1, head_dim)

time: 144 us -> 149 us (1.035)
  starting transfers between devices: 14.5 us -> 33.9 us
  waiting for transfers between devices: 26.7 us -> 11.2 us
    ppermute x0 -> x15, starting transfers between devices: none -> 20.7 us  [swapped_with_each(): outs.append(lax.ppermute(sent, axis, [(i, i ^ step) for i in range(size)]))]
    all_to_all x1 -> x0, waiting for transfers between devices: 7.68 us -> none  [local(): lax.all_to_all(copies_for(local_values), 'seq', split_axis=0, concat_axis...]
    all_to_all x1, waiting for transfers between devices: 6.76 us -> 0.01 us  [local(): lax.all_to_all(query_send, 'seq', split_axis=0, concat_axis=0, tiled=True)]
    all_to_all x1 -> x0, starting transfers between devices: 3.52 us -> none  [local(): lax.all_to_all(copies_for(local_values), 'seq', split_axis=0, concat_axis...]
    all_to_all x1, starting transfers between devices: 3.52 us -> 5.74 us  [local(): lax.all_to_all(copies_for(local_keys), 'seq', split_axis=0, concat_axis=0...]
  transfers between devices with their start and end apart: 5 -> 19, of which waited for: 4 -> 2; matrix products, arithmetic and copies ran while one was open for 1% -> 2% of each run, Pallas kernels for 0% -> 0%
where the time goes in v1:
time: 149 us
  blocking collectives  71.9 us (48%)
  starting transfers between devices  33.9 us (23%)
  matrix products  16.9 us (11%)
  waiting for transfers between devices  11.2 us (8%)
  other arithmetic  7.84 us (5%)
  local copies, waits for them, and re-layouts  6.28 us (4%)
    psum x1, blocking collectives, local(): mean_group = lax.psum(local_sum, 'seq') / entry_count  32.7 us
    psum x1, blocking collectives, local(): var_group = lax.psum(local_spread, 'seq') / entry_count  29.5 us
    ppermute x15, starting transfers between devices, swapped_with_each(): outs.append(lax.ppermute(sent, axis, [(i, i ^ step) for i in range(size)]))  20.7 us
    all_to_all x1, blocking collectives, local(): lax.all_to_all(head_result, 'seq', split_axis=0, concat_axis=0, tiled=True)  9.7 us
    all_to_all x1, waiting for transfers between devices, local(): lax.all_to_all(copies_for(local_keys), 'seq', split_axis=0, concat_axis=0...  7.14 us
    reduce_sum x2, other arithmetic, advance(): running_sum = running_sum * decay_by + jnp.sum(weights, axis=2)  6.15 us
    all_to_all x1, starting transfers between devices, local(): lax.all_to_all(copies_for(local_keys), 'seq', split_axis=0, concat_axis=0...  5.74 us
    dot_general x2, matrix products, advance(): jnp.einsum('qhd,khd->hqk', queries, keys_block, preferred_element_type=jn...  5.29 us
  transfers between devices with their start and end apart: 19, of which 2 were waited for; matrix products, arithmetic and copies ran while one was open for 2% of the time, Pallas kernels for 0%

profile of v1, /device:TPU:0, one launch (start us, length us, event | category | flops | bytes accessed | tf_op | source)
XLA Modules:
  0.0 148.7 jit_solution(14200220141715511863)
XLA Ops:
  0.0 2.7 %collective-permute-start = (bf16[128,320]{0,1:T(8,128)(2,1)}, bf16[128,320]{0,1:T(8,128)(2,1)S(1)}, u32[]{:S(2)}, u32[]{:S(2)}) collective-permute-start(bf16[128,320]{0,1:T(8,128)(2,1)} %param.17), channel_id=1, source_target_pairs={{0,1},{1,2},{2,3},{3,4},{4,5},{5,6},{6,7},{7,8},{8,9},{9,10},{10,1... | collective-permute-start | bytes 245768 | tf_op jit(solution)/shard_map/ppermute | solution.py:41
  2.7 1.3 collective-permute-start.1
  4.2 4.0 %collective-permute-done.1 = bf16[128,320]{0,1:T(8,128)(2,1)S(1)} collective-permute-done((bf16[128,320]{0,1:T(8,128)(2,1)}, bf16[128,320]{0,1:T(8,128)(2,1)S(1)}, u32[]{:S(2)}, u32[]{:S(2)}) %collective-permute-start.1) | collective-permute-done | bytes 81952 | tf_op jit(solution)/shard_map/ppermute | solution.py:44
  8.1 0.6 copy-done.9
  8.8 0.9 pad_maximum_fusion
  9.9 1.2 fusion.39
  11.2 1.9 %fusion.30 = f32[128,320]{0,1:T(8,128)} fusion(bf16[3,3,320,320]{3,2,1,0:T(8,128)(2,1)} %param.18, bf16[3,128,320]{2,1,0:T(8,128)(2,1)S(1)} %bitcast.206), kind=kOutput, calls=%fused_computation.47 | convolution fusion | flops 26214400 | bytes 655360 | tf_op jit(solution)/shard_map/dot_general | solution.py:59
  13.1 0.3 convolution_add_fusion.9
  13.4 0.3 convolution_add_fusion.8
  13.7 0.3 convolution_add_fusion.7
  14.0 0.3 convolution_add_fusion.6
  14.3 0.3 convolution_add_fusion.5
  14.6 0.3 convolution_add_fusion.4
  15.0 1.7 %fusion.79 = (f32[320]{0:T(512)S(1)}, f32[128,320]{0,1:T(8,128)S(1)}) fusion(f32[320]{0:T(512)S(1)} %copy-done.12, bf16[320,320]{1,0:T(8,128)(2,1)S(1)} %copy-done, f32[128,320]{0,1:T(8,128)} %fusion.30, f32[128,320]{0,1:T(8,128)S(1)} %convolution_add_fusion.4, bf16[128,320]{0,1:T(8,128)(2,1)} %copy-done.9, bf16[3,3,320,320]{3,2,1,0:T(8,128)(2,1)S(1)} %copy-done.2, ...), kind=kOutput, calls=%fused_computation.135 | convolution fusion | flops 53001920 | bytes 1152256 | tf_op jit(solution)/shard_map/dot_general | solution.py:118
  16.8 32.7 %psum.14 = f32[32]{0:T(128)S(1)} all-reduce(f32[32]{0:T(128)S(1)} %reduce_sum.63), channel_id=1, replica_groups=mesh['dp'=2,'seq'=16] {'seq'}, use_global_device_ids=true, to_apply=%region_2.3 | all-reduce | flops 32 | bytes 256 | tf_op jit(solution)/shard_map/psum | solution.py:124
  50.2 29.5 %psum.15 = f32[32]{0:T(128)S(1)} all-reduce(f32[32]{0:T(128)S(1)} %reduce_sum.66), channel_id=1, replica_groups=mesh['dp'=2,'seq'=16] {'seq'}, use_global_device_ids=true, to_apply=%region_5.6 | all-reduce | flops 32 | bytes 256 | tf_op jit(solution)/shard_map/psum | solution.py:127
  79.9 0.5 fusion.82
  80.6 1.2 convolution_convert_fusion
  82.1 1.8 %collective-permute-start.4 = (bf16[1,128,40]{1,2,0:T(8,128)(2,1)S(1)}, bf16[1,128,40]{1,2,0:T(8,128)(2,1)S(1)}, u32[]{:S(2)}, u32[]{:S(2)}) collective-permute-start(bf16[1,128,40]{1,2,0:T(8,128)(2,1)S(1)} %get-tuple-element.106), channel_id=1, source_target_pairs={{0,3},{1,2},{2,1},{3,0},{4,7},{5,6},{6,5},{7,4},{8,11},{9,10},{10,... | collective-permute-start | bytes 30728 | tf_op jit(solution)/shard_map/ppermute | solution.py:31
  83.9 1.7 %collective-permute-start.6 = (bf16[1,128,40]{1,2,0:T(8,128)(2,1)S(1)}, bf16[1,128,40]{1,2,0:T(8,128)(2,1)S(1)}, u32[]{:S(2)}, u32[]{:S(2)}) collective-permute-start(bf16[1,128,40]{1,2,0:T(8,128)(2,1)S(1)} %get-tuple-element.104), channel_id=1, source_target_pairs={{0,5},{1,4},{2,7},{3,6},{4,1},{5,0},{6,3},{7,2},{8,13},{9,12},{10,... | collective-permute-start | bytes 30728 | tf_op jit(solution)/shard_map/ppermute | solution.py:31
  85.6 0.3 convolution_convert_fusion.1
  86.0 0.8 reshape.157
  86.8 3.5 %all-to-all-start.1 = ((bf16[16,2,1280]{2,1,0:T(2,128)(2,1)}), bf16[16,2,1280]{2,1,0:T(2,128)(2,1)S(1)}, u32[]{:S(2)}, u32[]{:S(2)}) async-start(bf16[16,2,1280]{2,1,0:T(2,128)(2,1)} %reshape.157), calls=%async_computation.1 | async-start | bytes 163840 | tf_op jit(solution)/shard_map/all_to_all | solution.py:160
  90.4 0.3 convolution_convert_fusion.2
  90.7 2.8 %collective-permute-start.7 = (bf16[1,128,40]{1,2,0:T(8,128)(2,1)S(1)}, bf16[1,128,40]{1,2,0:T(8,128)(2,1)S(1)}, u32[]{:S(2)}, u32[]{:S(2)}) collective-permute-start(bf16[1,128,40]{1,2,0:T(8,128)(2,1)S(1)} %get-tuple-element.103), channel_id=1, source_target_pairs={{0,6},{1,7},{2,4},{3,5},{4,2},{5,3},{6,0},{7,1},{8,14},{9,15},{10,... | collective-permute-start | bytes 30728 | tf_op jit(solution)/shard_map/ppermute | solution.py:31
  93.5 2.5 %collective-permute-start.9 = (bf16[1,128,40]{1,2,0:T(8,128)(2,1)S(1)}, bf16[1,128,40]{1,2,0:T(8,128)(2,1)S(1)}, u32[]{:S(2)}, u32[]{:S(2)}) collective-permute-start(bf16[1,128,40]{1,2,0:T(8,128)(2,1)S(1)} %get-tuple-element.101), channel_id=1, source_target_pairs={{0,8},{1,9},{2,10},{3,11},{4,12},{5,13},{6,14},{7,15},{8,0},{9,1},... | collective-permute-start | bytes 30728 | tf_op jit(solution)/shard_map/ppermute | solution.py:31
  96.0 0.2 collective-permute-start.10
  96.3 3.5 %collective-permute-start.11 = (bf16[1,128,40]{1,2,0:T(8,128)(2,1)S(1)}, bf16[1,128,40]{1,2,0:T(8,128)(2,1)S(1)}, u32[]{:S(2)}, u32[]{:S(2)}) collective-permute-start(bf16[1,128,40]{1,2,0:T(8,128)(2,1)S(1)} %get-tuple-element.99), channel_id=1, source_target_pairs={{0,10},{1,11},{2,8},{3,9},{4,14},{5,15},{6,12},{7,13},{8,2},{9,3},... | collective-permute-start | bytes 30728 | tf_op jit(solution)/shard_map/ppermute | solution.py:31
  99.8 3.2 %collective-permute-start.13 = (bf16[1,128,40]{1,2,0:T(8,128)(2,1)S(1)}, bf16[1,128,40]{1,2,0:T(8,128)(2,1)S(1)}, u32[]{:S(2)}, u32[]{:S(2)}) collective-permute-start(bf16[1,128,40]{1,2,0:T(8,128)(2,1)S(1)} %get-tuple-element.97), channel_id=1, source_target_pairs={{0,12},{1,13},{2,14},{3,15},{4,8},{5,9},{6,10},{7,11},{8,4},{9,5},... | collective-permute-start | bytes 30728 | tf_op jit(solution)/shard_map/ppermute | solution.py:31
  103.1 0.4 collective-permute-start.14
  103.4 4.4 %collective-permute-start.15 = (bf16[1,128,40]{1,2,0:T(8,128)(2,1)S(1)}, bf16[1,128,40]{1,2,0:T(8,128)(2,1)S(1)}, u32[]{:S(2)}, u32[]{:S(2)}) collective-permute-start(bf16[1,128,40]{1,2,0:T(8,128)(2,1)S(1)} %get-tuple-element.95), channel_id=1, source_target_pairs={{0,14},{1,15},{2,12},{3,13},{4,10},{5,11},{6,8},{7,9},{8,6},{9,7},... | collective-permute-start | bytes 30728 | tf_op jit(solution)/shard_map/ppermute | solution.py:31
  108.0 0.7 broadcast_in_dim.19
  108.7 5.7 %all-to-all-start = ((bf16[16,128,40]{1,2,0:T(8,128)(2,1)}), bf16[16,128,40]{1,2,0:T(8,128)(2,1)S(1)}, u32[]{:S(2)}, u32[]{:S(2)}) async-start(bf16[16,128,40]{1,2,0:T(8,128)(2,1)} %bitcast.18), calls=%async_computation | async-start | bytes 327680 | tf_op jit(solution)/shard_map/all_to_all | solution.py:162
  114.5 0.6 gather_fusion
  115.0 0.3 copy.80
  115.7 7.1 %all-to-all-done = bf16[16,128,40]{1,2,0:T(8,128)(2,1)S(1)} async-done(((bf16[16,128,40]{1,2,0:T(8,128)(2,1)}), bf16[16,128,40]{1,2,0:T(8,128)(2,1)S(1)}, u32[]{:S(2)}, u32[]{:S(2)}) %all-to-all-start) | async-done | bytes 163872 | tf_op jit(solution)/shard_map/all_to_all | solution.py:162
  122.8 0.3 copy.79
  123.1 13.9 %while.15 = (s32[]{:T(128)}, f32[1,1024]{1,0:T(1,128)S(1)}, f32[1,1024]{1,0:T(1,128)S(1)}, f32[1024,1,40]{0,2,1:T(8,128)S(1)}, bf16[2,1024,40]{2,1,0:T(8,128)(2,...) while((s32[]{:T(128)}, f32[1,1024]{1,0:T(1,128)S(1)}, ...), condition=%wide.region_11.12_spmd.clone, body=%wide.region_8.0_spmd.clone.sunk | while | flops 176288768 | bytes 30359692 | solution.py:92
  123.1 2.6 %multiply_reduce_fusion.4 = (f32[1024]{0:T(1024)S(1)}, f32[1024,1024]{1,0:T(8,128)}) fusion(bf16[1024,1,40]{0,2,1:T(8,128)(2,1)S(1)} %get-tuple-element.188, bf16[2,1024,40]{2,1,0:T(8,128)(2,1)S(1)} %get-tuple-element.187, s32[]{:T(128)} %get-tuple-element.174), kind=kOutput, calls=%fused_computation.2.clone.1 | convolution fusion | flops 85982208 | bytes 4542468 | tf_op jit(solution)/shard_map/while/body/eval_jaxpr/qhd,khd->hqk/dot_general | solution.py:77
  125.8 3.1 %fusion.106 = f32[1024]{0:T(1024)S(1)} fusion(f32[1024,1024]{1,0:T(8,128)} %get-tuple-element.162, f32[1024]{0:T(1024)S(1)} %bitcast.213), kind=kLoop, calls=%fused_computation.4.clone.1 | loop fusion | flops 3144704 | bytes 4202496 | tf_op jit(solution)/shard_map/while/body/eval_jaxpr/reduce_sum | solution.py:83
  128.9 0.3 copy-done.1
  129.2 0.8 fusion.108
  130.1 2.6 %multiply_reduce_fusion.4 = (f32[1024]{0:T(1024)S(1)}, f32[1024,1024]{1,0:T(8,128)}) fusion(bf16[1024,1,40]{0,2,1:T(8,128)(2,1)S(1)} %get-tuple-element.188, bf16[2,1024,40]{2,1,0:T(8,128)(2,1)S(1)} %get-tuple-element.187, s32[]{:T(128)} %get-tuple-element.174), kind=kOutput, calls=%fused_computation.2.clone.1 | convolution fusion | flops 85982208 | bytes 4542468 | tf_op jit(solution)/shard_map/while/body/eval_jaxpr/qhd,khd->hqk/dot_general | solution.py:77
  132.8 3.1 %fusion.106 = f32[1024]{0:T(1024)S(1)} fusion(f32[1024,1024]{1,0:T(8,128)} %get-tuple-element.162, f32[1024]{0:T(1024)S(1)} %bitcast.213), kind=kLoop, calls=%fused_computation.4.clone.1 | loop fusion | flops 3144704 | bytes 4202496 | tf_op jit(solution)/shard_map/while/body/eval_jaxpr/reduce_sum | solution.py:83
  135.9 0.3 copy-done.1
  136.2 0.8 fusion.108
  137.5 9.7 %all_to_all.15 = bf16[16,2,1280]{2,1,0:T(2,128)(2,1)S(1)} all-to-all(bf16[16,2,1280]{2,1,0:T(2,128)(2,1)S(1)} %reshape.159), channel_id=1, replica_groups=mesh['dp'=2,'seq'=16] {'seq'}, dimensions={0} | all-to-all | bytes 163840 | tf_op jit(solution)/shard_map/all_to_all | solution.py:183
  147.6 1.1 fusion.28
  (106 shorter events, 3.4 us)
Async XLA Ops:
  0.0 14.9 %copy-start = (bf16[320,320]{1,0:T(8,128)(2,1)S(1)}, bf16[320,320]{1,0:T(8,128)(2,1)}, u32[]{:S(2)}) copy-start(bf16[320,320]{1,0:T(8,128)(2,1)} %param.20) | copy-start | bytes 614404
  0.0 13.1 %copy-start.2 = (bf16[3,3,320,320]{3,2,1,0:T(8,128)(2,1)S(1)}, bf16[3,3,320,320]{3,2,1,0:T(8,128)(2,1)}, u32[]{:S(2)}) copy-start(bf16[3,3,320,320]{3,2,1,0:T(8,128)(2,1)} %param.18) | copy-start | bytes 5529604
  0.0 4.2 %collective-permute-start = (bf16[128,320]{0,1:T(8,128)(2,1)}, bf16[128,320]{0,1:T(8,128)(2,1)S(1)}, u32[]{:S(2)}, u32[]{:S(2)}) collective-permute-start(bf16[128,320]{0,1:T(8,128)(2,1)} %param.17), channel_id=1, source_target_pairs={{0,1},{1,2},{2,3},{3,4},{4,5},{5,6},{6,7},{7,8},{8,9},{9,10},{10,1... | collective-permute-start | bytes 245768 | tf_op jit(solution)/shard_map/ppermute | solution.py:41
  2.7 5.5 %collective-permute-start.1 = (bf16[128,320]{0,1:T(8,128)(2,1)}, bf16[128,320]{0,1:T(8,128)(2,1)S(1)}, u32[]{:S(2)}, u32[]{:S(2)}) collective-permute-start(bf16[128,320]{0,1:T(8,128)(2,1)} %param.17), channel_id=1, source_target_pairs={{1,0},{2,1},{3,2},{4,3},{5,4},{6,5},{7,6},{8,7},{9,8},{10,9},{11,1... | collective-permute-start | bytes 245768 | tf_op jit(solution)/shard_map/ppermute | solution.py:44
  8.1 0.6 copy-start.9
  9.7 4.3 %copy-start.3 = (bf16[128,320]{0,1:T(8,128)(2,1)S(1)}, bf16[128,320]{0,1:T(8,128)(2,1)}, u32[]{:S(2)}) copy-start(bf16[128,320]{0,1:T(8,128)(2,1)} %param.17) | copy-start | bytes 245764
  13.4 1.5 %copy-start.12 = (f32[320]{0:T(512)S(1)}, f32[320]{0:T(512)}, u32[]{:S(2)}) copy-start(f32[320]{0:T(512)} %param.21) | copy-start | bytes 3844
  13.4 1.5 %copy-start.13 = (f32[320]{0:T(512)S(1)}, f32[320]{0:T(512)}, u32[]{:S(2)}) copy-start(f32[320]{0:T(512)} %param.19) | copy-start | bytes 3844
  14.0 65.9 %copy-start.4 = (bf16[320,320]{1,0:T(8,128)(2,1)S(1)}, bf16[320,320]{1,0:T(8,128)(2,1)}, u32[]{:S(2)}) copy-start(bf16[320,320]{1,0:T(8,128)(2,1)} %param.23) | copy-start | bytes 614404
  14.0 65.9 %copy-start.10 = (f32[320]{0:T(512)S(1)}, f32[320]{0:T(512)}, u32[]{:S(2)}) copy-start(f32[320]{0:T(512)} %param.22) | copy-start | bytes 3844
  14.3 66.1 %copy-start.11 = (f32[320]{0:T(512)S(1)}, f32[320]{0:T(512)}, u32[]{:S(2)}) copy-start(f32[320]{0:T(512)} %param.24) | copy-start | bytes 3844
  14.9 70.6 %copy-start.5 = (bf16[320,320]{1,0:T(8,128)(2,1)S(1)}, bf16[320,320]{1,0:T(8,128)(2,1)}, u32[]{:S(2)}) copy-start(bf16[320,320]{1,0:T(8,128)(2,1)} %param.25) | copy-start | bytes 614404
  16.6 73.7 %copy-start.6 = (bf16[320,320]{1,0:T(8,128)(2,1)S(1)}, bf16[320,320]{1,0:T(8,128)(2,1)}, u32[]{:S(2)}) copy-start(bf16[320,320]{1,0:T(8,128)(2,1)} %param.26) | copy-start | bytes 614404
  81.9 8.7 %collective-permute-start.2 = (bf16[1,128,40]{1,2,0:T(8,128)(2,1)S(1)}, bf16[1,128,40]{1,2,0:T(8,128)(2,1)S(1)}, u32[]{:S(2)}, u32[]{:S(2)}) collective-permute-start(bf16[1,128,40]{1,2,0:T(8,128)(2,1)S(1)} %get-tuple-element.108), channel_id=1, source_target_pairs={{0,1},{1,0},{2,3},{3,2},{4,5},{5,4},{6,7},{7,6},{8,9},{9,8},{10,11... | collective-permute-start | bytes 30728 | tf_op jit(solution)/shard_map/ppermute | solution.py:31
  82.0 11.5 %collective-permute-start.3 = (bf16[1,128,40]{1,2,0:T(8,128)(2,1)S(1)}, bf16[1,128,40]{1,2,0:T(8,128)(2,1)S(1)}, u32[]{:S(2)}, u32[]{:S(2)}) collective-permute-start(bf16[1,128,40]{1,2,0:T(8,128)(2,1)S(1)} %get-tuple-element.107), channel_id=1, source_target_pairs={{0,2},{1,3},{2,0},{3,1},{4,6},{5,7},{6,4},{7,5},{8,10},{9,11},{10,... | collective-permute-start | bytes 30728 | tf_op jit(solution)/shard_map/ppermute | solution.py:31
  82.1 11.4 %collective-permute-start.4 = (bf16[1,128,40]{1,2,0:T(8,128)(2,1)S(1)}, bf16[1,128,40]{1,2,0:T(8,128)(2,1)S(1)}, u32[]{:S(2)}, u32[]{:S(2)}) collective-permute-start(bf16[1,128,40]{1,2,0:T(8,128)(2,1)S(1)} %get-tuple-element.106), channel_id=1, source_target_pairs={{0,3},{1,2},{2,1},{3,0},{4,7},{5,6},{6,5},{7,4},{8,11},{9,10},{10,... | collective-permute-start | bytes 30728 | tf_op jit(solution)/shard_map/ppermute | solution.py:31
  83.9 12.1 %collective-permute-start.5 = (bf16[1,128,40]{1,2,0:T(8,128)(2,1)S(1)}, bf16[1,128,40]{1,2,0:T(8,128)(2,1)S(1)}, u32[]{:S(2)}, u32[]{:S(2)}) collective-permute-start(bf16[1,128,40]{1,2,0:T(8,128)(2,1)S(1)} %get-tuple-element.105), channel_id=1, source_target_pairs={{0,4},{1,5},{2,6},{3,7},{4,0},{5,1},{6,2},{7,3},{8,12},{9,13},{10,... | collective-permute-start | bytes 30728 | tf_op jit(solution)/shard_map/ppermute | solution.py:31
  83.9 12.4 %collective-permute-start.6 = (bf16[1,128,40]{1,2,0:T(8,128)(2,1)S(1)}, bf16[1,128,40]{1,2,0:T(8,128)(2,1)S(1)}, u32[]{:S(2)}, u32[]{:S(2)}) collective-permute-start(bf16[1,128,40]{1,2,0:T(8,128)(2,1)S(1)} %get-tuple-element.104), channel_id=1, source_target_pairs={{0,5},{1,4},{2,7},{3,6},{4,1},{5,0},{6,3},{7,2},{8,13},{9,12},{10,... | collective-permute-start | bytes 30728 | tf_op jit(solution)/shard_map/ppermute | solution.py:31
  86.8 21.1 %all-to-all-start.1 = ((bf16[16,2,1280]{2,1,0:T(2,128)(2,1)}), bf16[16,2,1280]{2,1,0:T(2,128)(2,1)S(1)}, u32[]{:S(2)}, u32[]{:S(2)}) async-start(bf16[16,2,1280]{2,1,0:T(2,128)(2,1)} %reshape.157), calls=%async_computation.1 | async-start | bytes 163840 | tf_op jit(solution)/shard_map/all_to_all | solution.py:160
  90.7 9.1 %collective-permute-start.7 = (bf16[1,128,40]{1,2,0:T(8,128)(2,1)S(1)}, bf16[1,128,40]{1,2,0:T(8,128)(2,1)S(1)}, u32[]{:S(2)}, u32[]{:S(2)}) collective-permute-start(bf16[1,128,40]{1,2,0:T(8,128)(2,1)S(1)} %get-tuple-element.103), channel_id=1, source_target_pairs={{0,6},{1,7},{2,4},{3,5},{4,2},{5,3},{6,0},{7,1},{8,14},{9,15},{10,... | collective-permute-start | bytes 30728 | tf_op jit(solution)/shard_map/ppermute | solution.py:31
  93.5 6.3 %collective-permute-start.8 = (bf16[1,128,40]{1,2,0:T(8,128)(2,1)S(1)}, bf16[1,128,40]{1,2,0:T(8,128)(2,1)S(1)}, u32[]{:S(2)}, u32[]{:S(2)}) collective-permute-start(bf16[1,128,40]{1,2,0:T(8,128)(2,1)S(1)} %get-tuple-element.102), channel_id=1, source_target_pairs={{0,7},{1,6},{2,5},{3,4},{4,3},{5,2},{6,1},{7,0},{8,15},{9,14},{10,... | collective-permute-start | bytes 30728 | tf_op jit(solution)/shard_map/ppermute | solution.py:31
  93.5 9.5 %collective-permute-start.9 = (bf16[1,128,40]{1,2,0:T(8,128)(2,1)S(1)}, bf16[1,128,40]{1,2,0:T(8,128)(2,1)S(1)}, u32[]{:S(2)}, u32[]{:S(2)}) collective-permute-start(bf16[1,128,40]{1,2,0:T(8,128)(2,1)S(1)} %get-tuple-element.101), channel_id=1, source_target_pairs={{0,8},{1,9},{2,10},{3,11},{4,12},{5,13},{6,14},{7,15},{8,0},{9,1},... | collective-permute-start | bytes 30728 | tf_op jit(solution)/shard_map/ppermute | solution.py:31
  96.0 7.4 %collective-permute-start.10 = (bf16[1,128,40]{1,2,0:T(8,128)(2,1)S(1)}, bf16[1,128,40]{1,2,0:T(8,128)(2,1)S(1)}, u32[]{:S(2)}, u32[]{:S(2)}) collective-permute-start(bf16[1,128,40]{1,2,0:T(8,128)(2,1)S(1)} %get-tuple-element.100), channel_id=1, source_target_pairs={{0,9},{1,8},{2,11},{3,10},{4,13},{5,12},{6,15},{7,14},{8,1},{9,0},... | collective-permute-start | bytes 30728 | tf_op jit(solution)/shard_map/ppermute | solution.py:31
  96.3 11.6 %collective-permute-start.11 = (bf16[1,128,40]{1,2,0:T(8,128)(2,1)S(1)}, bf16[1,128,40]{1,2,0:T(8,128)(2,1)S(1)}, u32[]{:S(2)}, u32[]{:S(2)}) collective-permute-start(bf16[1,128,40]{1,2,0:T(8,128)(2,1)S(1)} %get-tuple-element.99), channel_id=1, source_target_pairs={{0,10},{1,11},{2,8},{3,9},{4,14},{5,15},{6,12},{7,13},{8,2},{9,3},... | collective-permute-start | bytes 30728 | tf_op jit(solution)/shard_map/ppermute | solution.py:31
  99.8 8.2 %collective-permute-start.12 = (bf16[1,128,40]{1,2,0:T(8,128)(2,1)S(1)}, bf16[1,128,40]{1,2,0:T(8,128)(2,1)S(1)}, u32[]{:S(2)}, u32[]{:S(2)}) collective-permute-start(bf16[1,128,40]{1,2,0:T(8,128)(2,1)S(1)} %get-tuple-element.98), channel_id=1, source_target_pairs={{0,11},{1,10},{2,9},{3,8},{4,15},{5,14},{6,13},{7,12},{8,3},{9,2},... | collective-permute-start | bytes 30728 | tf_op jit(solution)/shard_map/ppermute | solution.py:31
  99.8 8.1 %collective-permute-start.13 = (bf16[1,128,40]{1,2,0:T(8,128)(2,1)S(1)}, bf16[1,128,40]{1,2,0:T(8,128)(2,1)S(1)}, u32[]{:S(2)}, u32[]{:S(2)}) collective-permute-start(bf16[1,128,40]{1,2,0:T(8,128)(2,1)S(1)} %get-tuple-element.97), channel_id=1, source_target_pairs={{0,12},{1,13},{2,14},{3,15},{4,8},{5,9},{6,10},{7,11},{8,4},{9,5},... | collective-permute-start | bytes 30728 | tf_op jit(solution)/shard_map/ppermute | solution.py:31
  103.1 4.9 %collective-permute-start.14 = (bf16[1,128,40]{1,2,0:T(8,128)(2,1)S(1)}, bf16[1,128,40]{1,2,0:T(8,128)(2,1)S(1)}, u32[]{:S(2)}, u32[]{:S(2)}) collective-permute-start(bf16[1,128,40]{1,2,0:T(8,128)(2,1)S(1)} %get-tuple-element.96), channel_id=1, source_target_pairs={{0,13},{1,12},{2,15},{3,14},{4,9},{5,8},{6,11},{7,10},{8,5},{9,4},... | collective-permute-start | bytes 30728 | tf_op jit(solution)/shard_map/ppermute | solution.py:31
  103.4 11.0 %collective-permute-start.15 = (bf16[1,128,40]{1,2,0:T(8,128)(2,1)S(1)}, bf16[1,128,40]{1,2,0:T(8,128)(2,1)S(1)}, u32[]{:S(2)}, u32[]{:S(2)}) collective-permute-start(bf16[1,128,40]{1,2,0:T(8,128)(2,1)S(1)} %get-tuple-element.95), channel_id=1, source_target_pairs={{0,14},{1,15},{2,12},{3,13},{4,10},{5,11},{6,8},{7,9},{8,6},{9,7},... | collective-permute-start | bytes 30728 | tf_op jit(solution)/shard_map/ppermute | solution.py:31
  107.8 6.6 %collective-permute-start.16 = (bf16[1,128,40]{1,2,0:T(8,128)(2,1)S(1)}, bf16[1,128,40]{1,2,0:T(8,128)(2,1)S(1)}, u32[]{:S(2)}, u32[]{:S(2)}) collective-permute-start(bf16[1,128,40]{1,2,0:T(8,128)(2,1)S(1)} %get-tuple-element.94), channel_id=1, source_target_pairs={{0,15},{1,14},{2,13},{3,12},{4,11},{5,10},{6,9},{7,8},{8,7},{9,6},... | collective-permute-start | bytes 30728 | tf_op jit(solution)/shard_map/ppermute | solution.py:31
  108.7 14.2 %all-to-all-start = ((bf16[16,128,40]{1,2,0:T(8,128)(2,1)}), bf16[16,128,40]{1,2,0:T(8,128)(2,1)S(1)}, u32[]{:S(2)}, u32[]{:S(2)}) async-start(bf16[16,128,40]{1,2,0:T(8,128)(2,1)} %bitcast.18), calls=%async_computation | async-start | bytes 327680 | tf_op jit(solution)/shard_map/all_to_all | solution.py:162
  125.8 3.4 %copy-start.1 = (f32[1024,1024]{1,0:T(8,128)S(1)}, f32[1024,1024]{1,0:T(8,128)}, u32[]{:S(2)}) copy-start(f32[1024,1024]{1,0:T(8,128)} %get-tuple-element.162) | copy-start | bytes 12582916 | tf_op jit(solution)/shard_map/while
  132.7 3.4 %copy-start.1 = (f32[1024,1024]{1,0:T(8,128)S(1)}, f32[1024,1024]{1,0:T(8,128)}, u32[]{:S(2)}) copy-start(f32[1024,1024]{1,0:T(8,128)} %get-tuple-element.162) | copy-start | bytes 12582916 | tf_op jit(solution)/shard_map/while
  137.1 10.6 %copy-start.7 = (bf16[320,320]{1,0:T(8,128)(2,1)S(1)}, bf16[320,320]{1,0:T(8,128)(2,1)}, u32[]{:S(2)}) copy-start(bf16[320,320]{1,0:T(8,128)(2,1)} %param.29) | copy-start | bytes 614404
  137.1 10.5 %copy-start.8 = (bf16[320,320]{1,0:T(8,128)(2,1)S(1)}, bf16[320,320]{1,0:T(8,128)(2,1)}, u32[]{:S(2)}) copy-start(bf16[320,320]{1,0:T(8,128)(2,1)} %param.28) | copy-start | bytes 614404
